TPU v7x, 32 devices: a whole 2x2x4 slice. The times are simulated.
32 devices in a mesh: gx: 4 (over z), gy: 2 (over y), gz: 4 (over x, core).
Axes of the slice: x: 2, y: 2, z: 4, core: 2. Of those that a mesh axis runs over, the one named last changes fastest.
Arguments:
- atom_x: float32 [4, 8, 256], P('gx', ('gy', 'gz')), may hold values from 0 to 95.99
- atom_y: float32 [4, 8, 256], P('gx', ('gy', 'gz')), may hold values from 0 to 47.99
- atom_z: float32 [4, 8, 256], P('gx', ('gy', 'gz')), may hold values from 0 to 384
- charges: float32 [4, 8, 256], P('gx', ('gy', 'gz')), may hold values from -4.5 to 4.5
- counts: int32 [4, 8], P('gx', ('gy', 'gz')), may hold values from 32 to 256, as said below
- background: float32 [384, 384, 384], P(('gy', 'gz'), 'gx'), may hold values from -0.3125 to 0.3125
Outputs:
- forces: float32 [3, 4, 8, 256], P(None, 'gx', ('gy', 'gz'))
Inputs may be any that keep to these rules, and one draw needn't show every extreme that they name: `counts`: live slots come first in each pencil; some pencil is full in every draw.
All inputs are finite; a program needn't handle non-finite values.
Results may differ from a plain program's by a relative error of at most 0.0003.
Values sent between devices are 32-bit elements; how exact they have to be, the bound alone decides.
No kernel may reach another device: no remote copies, remote signals or barrier semaphores. Data moves between devices by JAX's collectives and lax.ppermute only.
A program may use at most 128 MiB of HBM per device.

v0:
```python
import math
import jax
import jax.numpy as jnp
from jax import lax
from jax.sharding import PartitionSpec as P

COULOMB = 6.5
EWALD_BETA = 1.0
PRECISE = lax.Precision.HIGHEST


def extended(block, sides, width):
    for axis, dim in sides:
        count = lax.axis_size(axis)
        forward = [(i, i + 1) for i in range(count - 1)]
        forward.append((count - 1, 0))
        backward = [(target, source) for source, target in forward]
        low = lax.ppermute(
            lax.slice_in_dim(block, block.shape[dim] - width, None, axis=dim), axis, forward
        )
        high = lax.ppermute(lax.slice_in_dim(block, 0, width, axis=dim), axis, backward)
        block = jnp.concatenate([low, block, high], axis=dim)
    return block


def spline(offset):
    distance = jnp.minimum(offset, 5.0 - offset)
    ramp_zero = jax.nn.relu(distance)
    ramp_one = jax.nn.relu(distance - 1.0)
    ramp_two = jax.nn.relu(distance - 2.0)
    cube_zero = ramp_zero * ramp_zero * ramp_zero
    cube_one = ramp_one * ramp_one * ramp_one
    cube_two = ramp_two * ramp_two * ramp_two
    height = (cube_zero * ramp_zero - 5.0 * cube_one * ramp_one + 10.0 * cube_two * ramp_two) / 24.0
    gradient = (cube_zero - 5.0 * cube_one + 10.0 * cube_two) / 6.0
    return (height, jnp.where(offset < 2.5, gradient, -gradient))


def weights(coord_x, coord_y, coord_z, cells_x, cells_y, depth):
    edge_x = jnp.arange(cells_x + 4).astype(jnp.float32)
    weight_x, slope_x = spline(coord_x[None, :] - edge_x[:, None] + 4.5)
    edge_y = jnp.arange(cells_y + 4).astype(jnp.float32)
    weight_y, slope_y = spline(coord_y[None, :] - edge_y[:, None] + 4.5)
    planes = jnp.arange(depth).astype(jnp.float32)
    halfway = depth / 2.0
    offset_z = jnp.mod(coord_z[:, None] - planes[None, :] + halfway, float(depth)) - halfway + 2.5
    weight_z, slope_z = spline(offset_z)
    return (weight_x, slope_x, weight_y, slope_y, weight_z, slope_z)


def deposit(stencil, charge_live):
    weight_x, slope_x, weight_y, slope_y, weight_z, slope_z = stencil
    mixed = weight_y[:, None, :] * weight_x[None, :, :] * charge_live[None, None, :]
    flat = mixed.reshape(-1, charge_live.shape[0])
    spread = jnp.dot(flat, weight_z, precision=PRECISE, preferred_element_type=jnp.float32)
    return spread.reshape(weight_y.shape[0], weight_x.shape[0], weight_z.shape[1])


def pull(potential, stencil, charge_live):
    weight_x, slope_x, weight_y, slope_y, weight_z, slope_z = stencil
    extent_y, extent_x, depth = potential.shape
    flat = potential.reshape(extent_y * extent_x, depth)
    dims = (((1,), (1,)), ((), ()))
    plain = lax.dot_general(
        flat, weight_z, dims, precision=PRECISE, preferred_element_type=jnp.float32
    )
    deriv = lax.dot_general(
        flat, slope_z, dims, precision=PRECISE, preferred_element_type=jnp.float32
    )
    plain = plain.reshape(extent_y, extent_x, -1)
    deriv = deriv.reshape(extent_y, extent_x, -1)
    along_x = jnp.sum(weight_x[None] * plain, axis=1)
    turned_x = jnp.sum(slope_x[None] * plain, axis=1)
    depth_x = jnp.sum(weight_x[None] * deriv, axis=1)
    force_x = -charge_live * jnp.sum(weight_y * turned_x, axis=0)
    force_y = -charge_live * jnp.sum(slope_y * along_x, axis=0)
    force_z = -charge_live * jnp.sum(weight_y * depth_x, axis=0)
    return jnp.stack([force_x, force_y, force_z])


def modulus(indices, length):
    angles = 2.0 * math.pi / length * indices.astype(jnp.float32)
    return (230.0 + 152.0 * jnp.cos(angles) + 2.0 * jnp.cos(2.0 * angles)) / 384.0


def frequency(indices, length):
    signed = jnp.where(indices <= length // 2, indices, indices - length)
    return signed.astype(jnp.float32) / length


def influence(wave_z, wave_x, wave_y, depth, width_x, width_y):
    freq_z = frequency(wave_z, depth)
    freq_x = frequency(wave_x, width_x)
    freq_y = frequency(wave_y, width_y)
    square = freq_z[:, None, None] ** 2 + freq_x[None, :, None] ** 2 + freq_y[None, None, :] ** 2
    damping = (
        modulus(wave_z, depth)[:, None, None]
        * modulus(wave_x, width_x)[None, :, None]
        * modulus(wave_y, width_y)[None, None, :]
    )
    bounded = jnp.where(square > 0.0, square, 1.0)
    factor = COULOMB / (math.pi * width_x * width_y * depth)
    green = (
        factor * jnp.exp(-((math.pi / EWALD_BETA) ** 2) * square) / (bounded * damping * damping)
    )
    return jnp.where(square > 0.0, green, 0.0)


def tables(length):
    indices = jnp.arange(length)
    angles = jnp.mod(indices[:, None] * indices[None, :], length).astype(jnp.float32) * (
        2.0 * math.pi / length
    )
    return (jnp.cos(angles), jnp.sin(angles))


def depth_table(modes, length):
    wave_ids = jnp.arange(modes)
    cell_ids = jnp.arange(length)
    angles = jnp.mod(wave_ids[:, None] * cell_ids[None, :], length).astype(jnp.float32) * (
        2.0 * math.pi / length
    )
    return jnp.stack([jnp.cos(angles), -jnp.sin(angles)])


def complex_table(cosine, sine, sign):
    upper = jnp.stack([cosine, sign * sine], axis=1)
    lower = jnp.stack([-sign * sine, cosine], axis=1)
    return jnp.stack([upper, lower])


def per_device(atom_x, atom_y, atom_z, charges, counts, background):
    slots = atom_x.shape[-1]
    cells_y, cells_x, depth = background.shape
    parts_x = lax.axis_size("gx")
    parts_y = lax.axis_size(("gy", "gz"))
    width_x = cells_x * parts_x
    width_y = cells_y * parts_y
    live = jnp.arange(slots) < counts.reshape(())
    charge_live = jnp.where(live, charges.reshape(slots), 0.0)
    stencil = weights(
        atom_x.reshape(slots), atom_y.reshape(slots), atom_z.reshape(slots), cells_x, cells_y, depth
    )
    spread = deposit(stencil, charge_live)
    wide = extended(spread, (("gx", 1), (("gy", "gz"), 0)), 2)
    rows_done = (
        wide[4 : cells_y + 4].at[:2].add(wide[:2]).at[cells_y - 2 :].add(wide[cells_y + 6 :])
    )
    charge_grid = (
        rows_done[:, 4 : cells_x + 4]
        .at[:, :2]
        .add(rows_done[:, :2])
        .at[:, cells_x - 2 :]
        .add(rows_done[:, cells_x + 6 :])
    )
    charge_grid = charge_grid + background
    plane_count = (depth // 2 + 1 + parts_x - 1) // parts_x * parts_x
    wave_table = depth_table(plane_count, depth)
    cos_x, sin_x = tables(width_x)
    cos_y, sin_y = tables(width_y)
    ahead_x = complex_table(cos_x, sin_x, -1.0)
    ahead_y = complex_table(cos_y, sin_y, -1.0)
    back_x = complex_table(cos_x, sin_x, 1.0)
    back_y = complex_table(cos_y, sin_y, 1.0)
    spectrum = jnp.einsum("dkz,yxz->dkyx", wave_table, charge_grid, precision=PRECISE)

    def along_x(block):
        return jnp.einsum("ckyx,cxdm->dmky", block, ahead_x, precision=PRECISE)

    columns = along_x(lax.all_to_all(spectrum, "gx", split_axis=1, concat_axis=3, tiled=True))
    lines = jnp.einsum(
        "cxky,cydn->dnxk",
        lax.all_to_all(columns, ("gy", "gz"), split_axis=1, concat_axis=3, tiled=True),
        ahead_y,
        precision=PRECISE,
    )
    strip = lines.shape[2]
    planes = lines.shape[3]
    wave_z = lax.axis_index("gx") * planes + jnp.arange(planes)
    wave_x = lax.axis_index(("gy", "gz")) * strip + jnp.arange(strip)
    green = influence(wave_z, wave_x, jnp.arange(width_y), depth, width_x, width_y)
    edge_plane = (wave_z == 0) | (2 * wave_z == depth)
    plane_weight = jnp.where(edge_plane, 1.0, 2.0)
    plane_weight = jnp.where(2 * wave_z <= depth, plane_weight, 0.0)
    green = green * plane_weight[:, None, None]
    solved = lines * jnp.transpose(green, (2, 1, 0))[None]
    inverse = jnp.einsum("cnxk,cndy->dyxk", solved, back_y, precision=PRECISE)
    result = jnp.einsum(
        "cymk,cmdx->dxyk",
        lax.all_to_all(inverse, ("gy", "gz"), split_axis=1, concat_axis=2, tiled=True),
        back_x,
        precision=PRECISE,
    )
    potential = jnp.einsum(
        "dxyk,dkz->yxz",
        lax.all_to_all(result, "gx", split_axis=1, concat_axis=3, tiled=True),
        wave_table,
        precision=PRECISE,
    )
    potential = extended(potential, (("gx", 1), (("gy", "gz"), 0)), 2)
    forces = pull(potential, stencil, charge_live)
    return forces.reshape(3, 1, 1, slots)


def solution(mesh):
    in_specs = (
        P("gx", ("gy", "gz"), None),
        P("gx", ("gy", "gz"), None),
        P("gx", ("gy", "gz"), None),
        P("gx", ("gy", "gz"), None),
        P("gx", ("gy", "gz")),
        P(("gy", "gz"), "gx", None),
    )
    out_specs = P(None, "gx", ("gy", "gz"), None)
    return jax.shard_map(
        per_device, mesh=mesh, in_specs=in_specs, out_specs=out_specs, check_vma=False
    )
```

profile of v0, /device:TPU:0, one launch (start us, length us, event | category | flops | bytes accessed | tf_op | source)
XLA Modules:
  0.0 1233.9 jit_solution(1380806359779844134)
XLA Ops:
  40.9 17.3 %fusion.6 = f32[2,196,48,96]{1,3,2,0:T(8,128)} fusion(f32[48,96,384]{2,1,0:T(8,128)S(1)} %fusion.114, f32[48,96,384]{2,1,0:T(8,128)S(1)} %bitcast.132, f32[1,196,384]{2,1,0:T(8,128)S(1)} %get-tuple-element.77, f32[1,196,384]{2,1,0:T(8,128)S(1)} %get-tuple-element.78), kind=kOutput, calls=%fused_computation.12 | convolution fusion | flops 8325516288 | bytes 21983232 | tf_op jit(solution)/shard_map/dkz,yxz->dkyx/dot_general | solution.py:165
  81.4 205.0 %all-to-all-done = f32[2,196,48,96]{3,2,0,1:T(8,128)} async-done(((f32[2,196,48,96]{3,2,0,1:T(8,128)}), f32[2,196,48,96]{3,2,0,1:T(8,128)}, u32[]{:S(2)}, u32[]{:S(2)}) %all-to-all-start) | async-done | bytes 7225376 | tf_op jit(solution)/shard_map/all_to_all | solution.py:170
  311.6 24.0 %convolution_bitcast_fusion.1 = f32[2,384,49,48]{1,2,3,0:T(8,128)} fusion(f32[2,49,48,384,1]{3,1,0,2,4:T(8,128)} %reshape.633, f32[1,384,2,384]{3,1,0,2:T(8,128)S(1)} %get-tuple-element.67, f32[1,384,2,384]{3,1,0,2:T(8,128)} %get-tuple-element.70), kind=kOutput, calls=%fused_computation.32 | convolution fusion | flops 16647782400 | bytes 16809984 | tf_op jit(solution)/shard_map/ckyx,cxdm->dmky/dot_general | solution.py:168
  335.7 18.1 %copy.32 = f32[2,384,49,48]{2,3,0,1:T(8,128)} copy(f32[2,384,49,48]{1,2,3,0:T(8,128)} %convolution_bitcast_fusion.1) | data formatting | bytes 14450688 | tf_op jit(solution)/shard_map/ckyx,cxdm->dmky/dot_general | solution.py:168
  353.8 25.9 %reshape.651 = f32[8,1,225792]{2,1,0:T(1,128)} reshape(f32[384,2,48,49]{3,2,1,0:T(8,128)} %bitcast.123) | data formatting | bytes 14450688
  388.6 77.6 %all-to-all-done.1 = f32[8,1,225792]{2,1,0:T(1,128)} async-done(((f32[8,1,225792]{2,1,0:T(1,128)}), f32[8,1,225792]{2,1,0:T(1,128)}, u32[]{:S(2)}, u32[]{:S(2)}) %all-to-all-start.1) | async-done | bytes 7225376 | tf_op jit(solution)/shard_map/all_to_all | solution.py:173
  466.7 22.7 %reduce.8 = f32[8,225792]{1,0:T(8,128)} reduce(f32[8,1,225792]{2,1,0:T(1,128)} %all-to-all-done.1, f32[]{:T(128)} %broadcast.960), dimensions={1}, to_apply=%all_to_all.56.reduce_sub_computation | reduce | bytes 14450692 | tf_op jit(solution)/shard_map/all_to_all | solution.py:173
  489.4 36.5 %reshape.652 = f32[384,2,48,49]{3,2,1,0:T(8,128)} reshape(f32[8,225792]{1,0:T(8,128)} %reduce.8) | data formatting | bytes 14450688
  525.9 21.2 %copy.64 = f32[2,48,49,8,48]{4,3,2,0,1:T(8,128)} copy(f32[2,48,49,8,48]{2,4,0,1,3:T(8,128)} %bitcast.124) | data formatting | bytes 14450688 | tf_op jit(solution)/shard_map/all_to_all | solution.py:173
  563.3 25.2 %fusion.4 = f32[2,384,48,49,1]{1,3,4,0,2:T(8,128)S(1)} fusion(f32[2,48,49,384,1]{3,2,0,1,4:T(8,128)} %reshape.635, f32[1,384,2,384]{3,1,0,2:T(8,128)S(1)} %get-tuple-element.67, f32[1,384,2,384]{3,1,0,2:T(8,128)} %get-tuple-element.70), kind=kOutput, calls=%fused_computation.7 | convolution fusion | flops 16647782400 | bytes 16809984 | tf_op jit(solution)/shard_map/cxky,cydn->dnxk/dot_general | solution.py:171
  588.5 23.0 %fusion.20 = f32[2,384,48,49]{1,3,2,0:T(8,128)} fusion(f32[2,384,48,49,1]{1,3,4,0,2:T(8,128)S(1)} %fusion.4, f32[384,48,49]{0,2,1:T(8,128)S(1)} %copy-done, f32[1,384,2,384]{3,1,2,0:T(8,128)S(1)} %get-tuple-element.71, f32[1,384,2,384]{3,1,2,0:T(8,128)S(1)} %get-tuple-element.66), kind=kOutput, calls=%fused_computation.30 | convolution fusion | flops 16649588736 | bytes 20422656 | tf_op jit(solution)/shard_map/cnxk,cndy->dyxk/dot_general | solution.py:187
  611.4 18.1 %copy.37 = f32[2,384,48,49]{3,2,0,1:T(8,128)} copy(f32[2,384,48,49]{1,3,2,0:T(8,128)} %fusion.20) | data formatting | bytes 14450688 | tf_op jit(solution)/shard_map/cnxk,cndy->dyxk/dot_general | solution.py:187
  629.6 25.9 %reshape.653 = f32[8,1,225792]{2,1,0:T(1,128)} reshape(f32[384,2,48,49]{3,2,1,0:T(8,128)} %bitcast.125) | data formatting | bytes 14450688
  655.5 87.1 %all_to_all.72 = f32[8,1,225792]{2,1,0:T(1,128)} all-to-all(f32[8,1,225792]{2,1,0:T(1,128)} %reshape.653), channel_id=1, replica_groups=mesh['gx'=4,'gy'=2,'gz'=4] {'gy','gz'}, dimensions={0} | all-to-all | bytes 14450688 | tf_op jit(solution)/shard_map/all_to_all | solution.py:190
  742.6 22.4 %reduce.9 = f32[8,225792]{1,0:T(8,128)} reduce(f32[8,1,225792]{2,1,0:T(1,128)} %all_to_all.72, f32[]{:T(128)} %broadcast.960), dimensions={1}, to_apply=%all_to_all.60.reduce_sub_computation | reduce | bytes 14450692 | tf_op jit(solution)/shard_map/all_to_all | solution.py:190
  765.0 36.6 %reshape.654 = f32[384,2,48,49]{3,2,1,0:T(8,128)} reshape(f32[8,225792]{1,0:T(8,128)} %reduce.9) | data formatting | bytes 14450688
  801.6 21.2 %copy.67 = f32[2,48,8,48,49]{3,2,4,0,1:T(8,128)} copy(f32[2,48,8,48,49]{4,3,0,1,2:T(8,128)} %bitcast.126) | data formatting | bytes 14450688 | tf_op jit(solution)/shard_map/all_to_all | solution.py:190
  839.0 23.6 %convolution_bitcast_fusion = f32[2,384,48,49]{1,3,2,0:T(8,128)} fusion(f32[2,48,384,49,1]{2,3,0,1,4:T(8,128)} %reshape.641, f32[1,384,2,384]{3,1,2,0:T(8,128)S(1)} %get-tuple-element.71, f32[1,384,2,384]{3,1,2,0:T(8,128)S(1)} %get-tuple-element.66), kind=kOutput, calls=%fused_computation.31 | convolution fusion | flops 16647782400 | bytes 16809984 | tf_op jit(solution)/shard_map/cymk,cmdx->dxyk/dot_general | solution.py:188
  862.5 18.1 %copy.42 = f32[2,384,48,49]{3,2,0,1:T(8,128)} copy(f32[2,384,48,49]{1,3,2,0:T(8,128)} %convolution_bitcast_fusion) | data formatting | bytes 14450688 | tf_op jit(solution)/shard_map/cymk,cmdx->dxyk/dot_general | solution.py:188
  880.7 39.1 %reshape.655 = f32[4,1,451584]{2,1,0:T(1,128)} reshape(f32[384,2,48,49]{3,2,1,0:T(8,128)} %bitcast.127) | data formatting | bytes 14450688
  919.8 165.2 %all_to_all.73 = f32[4,1,451584]{2,1,0:T(1,128)} all-to-all(f32[4,1,451584]{2,1,0:T(1,128)} %reshape.655), channel_id=1, replica_groups=mesh['gx'=4,'gy'=2,'gz'=4] {'gx'}, dimensions={0} | all-to-all | bytes 14450688 | tf_op jit(solution)/shard_map/all_to_all | solution.py:196
  1085.1 24.1 %reduce.10 = f32[4,451584]{1,0:T(4,128)} reduce(f32[4,1,451584]{2,1,0:T(1,128)} %all_to_all.73, f32[]{:T(128)} %broadcast.960), dimensions={1}, to_apply=%all_to_all.64.reduce_sub_computation | reduce | bytes 14450692 | tf_op jit(solution)/shard_map/all_to_all | solution.py:196
  1109.1 37.4 %reshape.656 = f32[384,2,48,49]{3,2,1,0:T(8,128)} reshape(f32[4,451584]{1,0:T(4,128)} %reduce.10) | data formatting | bytes 14450688
  1167.9 21.7 %fusion.23 = f32[48,96,384]{2,1,0:T(8,128)S(1)} fusion(f32[2,96,48,196]{1,2,3,0:T(8,128)S(1)} %bitcast.129, f32[1,196,384]{2,1,0:T(8,128)S(1)} %copy-done.2, f32[1,196,384]{2,1,0:T(8,128)S(1)} %copy-done.4), kind=kOutput, calls=%fused_computation.33 | convolution fusion | flops 8323746816 | bytes 14905344 | tf_op jit(solution)/shard_map/dxyk,dkz->yxz/dot_general | solution.py:194
  (96 shorter events, 195.5 us)
Async XLA Ops:
  0.0 27.7 %copy-start.8 = (f32[384]{0:T(512)}, f32[384]{0:T(512)S(1)}, u32[]{:S(2)}) copy-start(f32[384]{0:T(512)S(1)} %iota_convert_fusion) | copy-start | bytes 4612
  2.2 25.5 %copy-start.5 = (f32[100,256]{1,0:T(8,128)}, f32[100,256]{1,0:T(8,128)S(1)}, u32[]{:S(2)}) copy-start(f32[100,256]{1,0:T(8,128)S(1)} %get-tuple-element.73) | copy-start | bytes 307204
  14.0 9.6 collective-permute-start.1
  19.1 7.7 collective-permute-start
  20.4 18.8 %copy-start.1 = (f32[1,196,384]{2,1,0:T(8,128)}, f32[1,196,384]{2,1,0:T(8,128)S(1)}, u32[]{:S(2)}) copy-start(f32[1,196,384]{2,1,0:T(8,128)S(1)} %get-tuple-element.77) | copy-start | bytes 903172
  20.4 18.8 %copy-start.3 = (f32[1,196,384]{2,1,0:T(8,128)}, f32[1,196,384]{2,1,0:T(8,128)S(1)}, u32[]{:S(2)}) copy-start(f32[1,196,384]{2,1,0:T(8,128)S(1)} %get-tuple-element.78) | copy-start | bytes 903172
  27.7 9.0 collective-permute-start.2
  27.7 10.1 collective-permute-start.3
  69.1 217.2 %all-to-all-start = ((f32[2,196,48,96]{3,2,0,1:T(8,128)}), f32[2,196,48,96]{3,2,0,1:T(8,128)}, u32[]{:S(2)}, u32[]{:S(2)}) async-start(f32[2,196,48,96]{3,2,0,1:T(8,128)} %copy.28), calls=%async_computation | async-start | bytes 19267584 | tf_op jit(solution)/shard_map/all_to_all | solution.py:170
  379.7 86.4 %all-to-all-start.1 = ((f32[8,1,225792]{2,1,0:T(1,128)}), f32[8,1,225792]{2,1,0:T(1,128)}, u32[]{:S(2)}, u32[]{:S(2)}) async-start(f32[8,1,225792]{2,1,0:T(1,128)} %reshape.651), calls=%async_computation.1 | async-start | bytes 14450688 | tf_op jit(solution)/shard_map/all_to_all | solution.py:173
  563.3 25.2 %copy-start = (f32[384,48,49]{0,2,1:T(8,128)S(1)}, f32[384,48,49]{0,2,1:T(8,128)}, u32[]{:S(2)}) copy-start(f32[384,48,49]{0,2,1:T(8,128)} %fusion.13) | copy-start | bytes 10838020
  1163.3 4.6 copy-start.2
  1163.3 4.6 copy-start.4
  1189.6 18.0 %copy-start.6 = (f32[100,256]{1,0:T(8,128)S(1)}, f32[100,256]{1,0:T(8,128)}, u32[]{:S(2)}) copy-start(f32[100,256]{1,0:T(8,128)} %copy-done.5) | copy-start | bytes 307204
  1189.6 18.0 %copy-start.9 = (f32[384]{0:T(512)S(1)}, f32[384]{0:T(512)}, u32[]{:S(2)}) copy-start(f32[384]{0:T(512)} %copy-done.8) | copy-start | bytes 4612
  1189.6 18.0 %copy-start.14 = (f32[1,1,256]{2,1,0:T(1,128)S(1)}, f32[1,1,256]{2,1,0:T(1,128)}, u32[]{:S(2)}) copy-start(f32[1,1,256]{2,1,0:T(1,128)} %param.16) | copy-start | bytes 3076
  1189.7 6.2 collective-permute-start.5
  1191.8 6.9 collective-permute-start.4
  1198.8 7.9 collective-permute-start.7
  1198.8 21.0 %copy-start.7 = (f32[100,256]{1,0:T(8,128)S(1)}, f32[100,256]{1,0:T(8,128)}, u32[]{:S(2)}) copy-start(f32[100,256]{1,0:T(8,128)} %get-tuple-element.72) | copy-start | bytes 307204
  1198.8 8.7 collective-permute-start.6
  1219.8 13.1 %copy-start.10 = (f32[1,1,256]{2,1,0:T(1,128)S(1)}, f32[1,1,256]{2,1,0:T(1,128)}, u32[]{:S(2)}) copy-start(f32[1,1,256]{2,1,0:T(1,128)} %param.15) | copy-start | bytes 3076
  1219.8 13.1 %copy-start.13 = (f32[52]{0:T(128)S(1)}, f32[52]{0:T(128)}, u32[]{:S(2)}) copy-start(f32[52]{0:T(128)} %copy-done.12) | copy-start | bytes 628
  1219.8 13.2 %copy-start.11 = (f32[1,1,256]{2,1,0:T(1,128)S(1)}, f32[1,1,256]{2,1,0:T(1,128)}, u32[]{:S(2)}) copy-start(f32[1,1,256]{2,1,0:T(1,128)} %param.17) | copy-start | bytes 3076
  (3 other events, 8.9 us)
where the time goes:
time: 1250 us; the launch traced here: 1230 us
  local copies, waits for them, and re-layouts  393 us (31%)
  waiting for transfers between devices  309 us (25%)
  blocking collectives  252 us (20%)
  matrix products  170 us (14%)
  other arithmetic  86.9 us (7%)
  starting transfers between devices  21.7 us (2%)
    all_to_all x1, waiting for transfers between devices, per_device(): lax.all_to_all(spectrum, 'gx', split_axis=1, concat_axis=3, tiled=True)  205 us
    unnamed x40, local copies, waits for them, and re-layouts  203 us
    all_to_all x1, blocking collectives, per_device(): lax.all_to_all(result, 'gx', split_axis=1, concat_axis=3, tiled=True)  165 us
    all_to_all x1, blocking collectives, per_device(): lax.all_to_all(inverse, ('gy', 'gz'), split_axis=1, concat_axis=2, tiled=...  87.1 us
    all_to_all x1, waiting for transfers between devices, per_device(): lax.all_to_all(columns, ('gy', 'gz'), split_axis=1, concat_axis=3, tiled=...  77.6 us
    all_to_all x3, local copies, waits for them, and re-layouts, per_device(): lax.all_to_all(columns, ('gy', 'gz'), split_axis=1, concat_axis=3, tiled=...  37.9 us
    all_to_all x2, local copies, waits for them, and re-layouts, per_device(): lax.all_to_all(inverse, ('gy', 'gz'), split_axis=1, concat_axis=2, tiled=...  37.4 us
    all_to_all x2, local copies, waits for them, and re-layouts, per_device(): lax.all_to_all(spectrum, 'gx', split_axis=1, concat_axis=3, tiled=True)  25.3 us
  transfers between devices with their start and end apart: 10, of which 9 were waited for; matrix products, arithmetic and copies ran while one was open for 1% of the time, Pallas kernels for 0%

commit v1 on v0

--- a/solution.py
+++ b/solution.py
@@ -193,7 +193,10 @@
     )
     potential = jnp.einsum(
         "dxyk,dkz->yxz",
-        lax.all_to_all(result, "gx", split_axis=1, concat_axis=3, tiled=True),
+        jnp.concatenate(
+            lax.all_to_all(jnp.stack(jnp.split(result, lax.axis_size("gx"), axis=1)), "gx", 0, 0),
+            axis=3,
+        ),
         wave_table,
         precision=PRECISE,
     )

time: 1250 us -> 1180 us (0.944)
  local copies, waits for them, and re-layouts: 393 us -> 298 us
  blocking collectives: 252 us -> 305 us
  other arithmetic: 86.9 us -> 67.1 us
    unnamed x40 -> x38, local copies, waits for them, and re-layouts: 203 us -> 127 us
    all_to_all x1, blocking collectives: 165 us -> 218 us  [per_device(): lax.all_to_all(jnp.stack(jnp.split(result, lax.axis_size('gx'), axis=1)),...]
    all_to_all x1 -> x0, other arithmetic: 24.1 us -> none  [per_device(): lax.all_to_all(result, 'gx', split_axis=1, concat_axis=3, tiled=True)]
    all_to_all x2 -> x0, local copies, waits for them, and re-layouts: 21.3 us -> none  [per_device(): lax.all_to_all(result, 'gx', split_axis=1, concat_axis=3, tiled=True)]
    dot_general x1 -> x0, local copies, waits for them, and re-layouts: 18.1 us -> none  [per_device(): jnp.einsum('cymk,cmdx->dxyk', lax.all_to_all(inverse, ('gy', 'gz'), split...]
    another operation x0 -> x2, local copies, waits for them, and re-layouts: none -> 16.7 us  [per_device(): jnp.stack(jnp.split(result, lax.axis_size('gx'), axis=1))]
where the time goes in v1:
time: 1180 us; the launch traced here: 1170 us
  waiting for transfers between devices  309 us (26%)
  blocking collectives  305 us (26%)
  local copies, waits for them, and re-layouts  298 us (25%)
  matrix products  171 us (14%)
  other arithmetic  67.1 us (6%)
  starting transfers between devices  21.8 us (2%)
    all_to_all x1, blocking collectives, per_device(): lax.all_to_all(jnp.stack(jnp.split(result, lax.axis_size('gx'), axis=1)),...  218 us
    all_to_all x1, waiting for transfers between devices, per_device(): lax.all_to_all(spectrum, 'gx', split_axis=1, concat_axis=3, tiled=True)  205 us
    unnamed x38, local copies, waits for them, and re-layouts  127 us
    all_to_all x1, blocking collectives, per_device(): lax.all_to_all(inverse, ('gy', 'gz'), split_axis=1, concat_axis=2, tiled=...  87.1 us
    all_to_all x1, waiting for transfers between devices, per_device(): lax.all_to_all(columns, ('gy', 'gz'), split_axis=1, concat_axis=3, tiled=...  77.5 us
    all_to_all x3, local copies, waits for them, and re-layouts, per_device(): lax.all_to_all(columns, ('gy', 'gz'), split_axis=1, concat_axis=3, tiled=...  37.9 us
    all_to_all x2, local copies, waits for them, and re-layouts, per_device(): lax.all_to_all(inverse, ('gy', 'gz'), split_axis=1, concat_axis=2, tiled=...  37.3 us
    all_to_all x2, local copies, waits for them, and re-layouts, per_device(): lax.all_to_all(spectrum, 'gx', split_axis=1, concat_axis=3, tiled=True)  25.3 us
  transfers between devices with their start and end apart: 10, of which 9 were waited for; matrix products, arithmetic and copies ran while one was open for 1% of the time, Pallas kernels for 0%

profile of v1, /device:TPU:0, one launch (start us, length us, event | category | flops | bytes accessed | tf_op | source)
XLA Modules:
  0.0 1172.4 jit_solution(16861791548499330366)
XLA Ops:
  40.9 17.4 %fusion.6 = f32[2,196,48,96]{1,3,2,0:T(8,128)} fusion(f32[48,96,384]{2,1,0:T(8,128)S(1)} %fusion.114, f32[48,96,384]{2,1,0:T(8,128)S(1)} %bitcast.135, f32[1,196,384]{2,1,0:T(8,128)S(1)} %get-tuple-element.81, f32[1,196,384]{2,1,0:T(8,128)S(1)} %get-tuple-element.82), kind=kOutput, calls=%fused_computation.13 | convolution fusion | flops 8325516288 | bytes 21983232 | tf_op jit(solution)/shard_map/dkz,yxz->dkyx/dot_general | solution.py:165
  81.5 205.0 %all-to-all-done = f32[2,196,48,96]{3,2,0,1:T(8,128)} async-done(((f32[2,196,48,96]{3,2,0,1:T(8,128)}), f32[2,196,48,96]{3,2,0,1:T(8,128)}, u32[]{:S(2)}, u32[]{:S(2)}) %all-to-all-start) | async-done | bytes 7225376 | tf_op jit(solution)/shard_map/all_to_all | solution.py:170
  286.5 13.6 %copy.58 = f32[2,49,48,4,96]{4,3,1,0,2:T(4,128)} copy(f32[2,49,48,4,96]{4,2,0,1,3:T(8,128)} %bitcast.21) | data formatting | bytes 14450688 | tf_op jit(solution)/shard_map/all_to_all | solution.py:170
  311.8 24.1 %convolution_bitcast_fusion.1 = f32[2,384,49,48]{1,2,3,0:T(8,128)} fusion(f32[2,49,48,384,1]{3,1,0,2,4:T(8,128)} %reshape.641, f32[1,384,2,384]{3,1,0,2:T(8,128)S(1)} %get-tuple-element.71, f32[1,384,2,384]{3,1,0,2:T(8,128)} %get-tuple-element.74), kind=kOutput, calls=%fused_computation.33 | convolution fusion | flops 16647782400 | bytes 16809984 | tf_op jit(solution)/shard_map/ckyx,cxdm->dmky/dot_general | solution.py:168
  335.9 18.1 %copy.30 = f32[2,384,49,48]{2,3,0,1:T(8,128)} copy(f32[2,384,49,48]{1,2,3,0:T(8,128)} %convolution_bitcast_fusion.1) | data formatting | bytes 14450688 | tf_op jit(solution)/shard_map/ckyx,cxdm->dmky/dot_general | solution.py:168
  354.0 25.9 %reshape.659 = f32[8,1,225792]{2,1,0:T(1,128)} reshape(f32[384,2,48,49]{3,2,1,0:T(8,128)} %bitcast.128) | data formatting | bytes 14450688
  388.8 77.5 %all-to-all-done.1 = f32[8,1,225792]{2,1,0:T(1,128)} async-done(((f32[8,1,225792]{2,1,0:T(1,128)}), f32[8,1,225792]{2,1,0:T(1,128)}, u32[]{:S(2)}, u32[]{:S(2)}) %all-to-all-start.1) | async-done | bytes 7225376 | tf_op jit(solution)/shard_map/all_to_all | solution.py:173
  466.9 22.6 %reduce.8 = f32[8,225792]{1,0:T(8,128)} reduce(f32[8,1,225792]{2,1,0:T(1,128)} %all-to-all-done.1, f32[]{:T(128)} %broadcast.960), dimensions={1}, to_apply=%all_to_all.46.reduce_sub_computation | reduce | bytes 14450692 | tf_op jit(solution)/shard_map/all_to_all | solution.py:173
  489.6 36.5 %reshape.660 = f32[384,2,48,49]{3,2,1,0:T(8,128)} reshape(f32[8,225792]{1,0:T(8,128)} %reduce.8) | data formatting | bytes 14450688
  526.1 21.1 %copy.61 = f32[2,48,49,8,48]{4,3,2,0,1:T(8,128)} copy(f32[2,48,49,8,48]{2,4,0,1,3:T(8,128)} %bitcast.129) | data formatting | bytes 14450688 | tf_op jit(solution)/shard_map/all_to_all | solution.py:173
  547.3 16.2 %reshape.643 = f32[2,48,49,384,1]{3,2,0,1,4:T(8,128)} reshape(f32[2,48,49,8,48]{4,3,2,0,1:T(8,128)} %copy.61) | data formatting | bytes 14450688 | tf_op jit(solution)/shard_map/all_to_all | solution.py:173
  563.5 25.2 %fusion.4 = f32[2,384,48,49,1]{1,3,4,0,2:T(8,128)S(1)} fusion(f32[2,48,49,384,1]{3,2,0,1,4:T(8,128)} %reshape.643, f32[1,384,2,384]{3,1,0,2:T(8,128)S(1)} %get-tuple-element.71, f32[1,384,2,384]{3,1,0,2:T(8,128)} %get-tuple-element.74), kind=kOutput, calls=%fused_computation.8 | convolution fusion | flops 16647782400 | bytes 16809984 | tf_op jit(solution)/shard_map/cxky,cydn->dnxk/dot_general | solution.py:171
  588.6 23.0 %fusion.20 = f32[2,384,48,49]{1,3,2,0:T(8,128)} fusion(f32[2,384,48,49,1]{1,3,4,0,2:T(8,128)S(1)} %fusion.4, f32[384,48,49]{0,2,1:T(8,128)S(1)} %copy-done, f32[1,384,2,384]{3,1,2,0:T(8,128)S(1)} %get-tuple-element.75, f32[1,384,2,384]{3,1,2,0:T(8,128)S(1)} %get-tuple-element.70), kind=kOutput, calls=%fused_computation.31 | convolution fusion | flops 16649588736 | bytes 20422656 | tf_op jit(solution)/shard_map/cnxk,cndy->dyxk/dot_general | solution.py:187
  611.7 18.1 %copy.35 = f32[2,384,48,49]{3,2,0,1:T(8,128)} copy(f32[2,384,48,49]{1,3,2,0:T(8,128)} %fusion.20) | data formatting | bytes 14450688 | tf_op jit(solution)/shard_map/cnxk,cndy->dyxk/dot_general | solution.py:187
  629.8 25.9 %reshape.661 = f32[8,1,225792]{2,1,0:T(1,128)} reshape(f32[384,2,48,49]{3,2,1,0:T(8,128)} %bitcast.130) | data formatting | bytes 14450688
  655.7 87.1 %all_to_all.59 = f32[8,1,225792]{2,1,0:T(1,128)} all-to-all(f32[8,1,225792]{2,1,0:T(1,128)} %reshape.661), channel_id=1, replica_groups=mesh['gx'=4,'gy'=2,'gz'=4] {'gy','gz'}, dimensions={0} | all-to-all | bytes 14450688 | tf_op jit(solution)/shard_map/all_to_all | solution.py:190
  742.8 22.4 %reduce.9 = f32[8,225792]{1,0:T(8,128)} reduce(f32[8,1,225792]{2,1,0:T(1,128)} %all_to_all.59, f32[]{:T(128)} %broadcast.960), dimensions={1}, to_apply=%all_to_all.50.reduce_sub_computation | reduce | bytes 14450692 | tf_op jit(solution)/shard_map/all_to_all | solution.py:190
  765.2 36.8 %reshape.662 = f32[384,2,48,49]{3,2,1,0:T(8,128)} reshape(f32[8,225792]{1,0:T(8,128)} %reduce.9) | data formatting | bytes 14450688
  802.0 21.1 %copy.64 = f32[2,48,8,48,49]{3,2,4,0,1:T(8,128)} copy(f32[2,48,8,48,49]{4,3,0,1,2:T(8,128)} %bitcast.131) | data formatting | bytes 14450688 | tf_op jit(solution)/shard_map/all_to_all | solution.py:190
  823.1 16.2 %reshape.649 = f32[2,48,384,49,1]{2,3,0,1,4:T(8,128)} reshape(f32[2,48,8,48,49]{3,2,4,0,1:T(8,128)} %copy.64) | data formatting | bytes 14450688 | tf_op jit(solution)/shard_map/all_to_all | solution.py:190
  839.3 23.6 %convolution_bitcast_fusion = f32[2,384,48,49]{1,3,2,0:T(8,128)} fusion(f32[2,48,384,49,1]{2,3,0,1,4:T(8,128)} %reshape.649, f32[1,384,2,384]{3,1,2,0:T(8,128)S(1)} %get-tuple-element.75, f32[1,384,2,384]{3,1,2,0:T(8,128)S(1)} %get-tuple-element.70), kind=kOutput, calls=%fused_computation.32 | convolution fusion | flops 16647782400 | bytes 16809984 | tf_op jit(solution)/shard_map/cymk,cmdx->dxyk/dot_general | solution.py:188
  883.8 217.7 %all_to_all.60 = f32[4,2,96,48,49]{2,3,4,1,0:T(8,128)} all-to-all(f32[4,2,96,48,49]{2,3,4,1,0:T(8,128)} %copy.40), channel_id=1, replica_groups=mesh['gx'=4,'gy'=2,'gz'=4] {'gx'}, dimensions={0} | all-to-all | bytes 14450688 | tf_op jit(solution)/shard_map/all_to_all | solution.py:197
  1106.1 21.7 %fusion.23 = f32[48,96,384]{2,1,0:T(8,128)S(1)} fusion(f32[2,96,48,196]{1,2,3,0:T(8,128)S(1)} %bitcast.132, f32[1,196,384]{2,1,0:T(8,128)S(1)} %copy-done.2, f32[1,196,384]{2,1,0:T(8,128)S(1)} %copy-done.4), kind=kOutput, calls=%fused_computation.34 | convolution fusion | flops 8323746816 | bytes 14905344 | tf_op jit(solution)/shard_map/dxyk,dkz->yxz/dot_general | solution.py:194
  1158.0 13.1 %multiply_reduce_fusion.2 = (f32[52,256]{1,0:T(8,128)S(1)}, f32[52,256]{1,0:T(8,128)S(1)}) fusion(f32[100,256]{1,0:T(8,128)S(1)} %copy-done.7, f32[100,256]{1,0:T(8,128)S(1)} %copy-done.6, f32[384]{0:T(512)S(1)} %copy-done.9, f32[256]{0:T(256)S(1)} %bitcast.145, f32[2,100,384]{2,1,0:T(8,128)S(1)} %collective-permute-done.7, ...), kind=kOutput, calls=%fused_computation.19 | convolution fusion | flops 6150404096 | bytes 8301056 | tf_op jit(solution)/shard_map/dot_general | solution.py:64
  (94 shorter events, 140.7 us)
Async XLA Ops:
  0.0 27.7 %copy-start.8 = (f32[384]{0:T(512)}, f32[384]{0:T(512)S(1)}, u32[]{:S(2)}) copy-start(f32[384]{0:T(512)S(1)} %iota_convert_fusion) | copy-start | bytes 4612
  2.2 25.6 %copy-start.5 = (f32[100,256]{1,0:T(8,128)}, f32[100,256]{1,0:T(8,128)S(1)}, u32[]{:S(2)}) copy-start(f32[100,256]{1,0:T(8,128)S(1)} %get-tuple-element.77) | copy-start | bytes 307204
  14.0 9.6 collective-permute-start.1
  19.1 7.7 collective-permute-start
  20.4 18.8 %copy-start.1 = (f32[1,196,384]{2,1,0:T(8,128)}, f32[1,196,384]{2,1,0:T(8,128)S(1)}, u32[]{:S(2)}) copy-start(f32[1,196,384]{2,1,0:T(8,128)S(1)} %get-tuple-element.81) | copy-start | bytes 903172
  20.4 18.8 %copy-start.3 = (f32[1,196,384]{2,1,0:T(8,128)}, f32[1,196,384]{2,1,0:T(8,128)S(1)}, u32[]{:S(2)}) copy-start(f32[1,196,384]{2,1,0:T(8,128)S(1)} %get-tuple-element.82) | copy-start | bytes 903172
  27.7 9.0 collective-permute-start.2
  27.7 10.0 collective-permute-start.3
  69.2 217.3 %all-to-all-start = ((f32[2,196,48,96]{3,2,0,1:T(8,128)}), f32[2,196,48,96]{3,2,0,1:T(8,128)}, u32[]{:S(2)}, u32[]{:S(2)}) async-start(f32[2,196,48,96]{3,2,0,1:T(8,128)} %copy.26), calls=%async_computation | async-start | bytes 19267584 | tf_op jit(solution)/shard_map/all_to_all | solution.py:170
  379.9 86.4 %all-to-all-start.1 = ((f32[8,1,225792]{2,1,0:T(1,128)}), f32[8,1,225792]{2,1,0:T(1,128)}, u32[]{:S(2)}, u32[]{:S(2)}) async-start(f32[8,1,225792]{2,1,0:T(1,128)} %reshape.659), calls=%async_computation.1 | async-start | bytes 14450688 | tf_op jit(solution)/shard_map/all_to_all | solution.py:173
  563.5 25.2 %copy-start = (f32[384,48,49]{0,2,1:T(8,128)S(1)}, f32[384,48,49]{0,2,1:T(8,128)}, u32[]{:S(2)}) copy-start(f32[384,48,49]{0,2,1:T(8,128)} %fusion.13) | copy-start | bytes 10838020
  1101.5 4.5 copy-start.2
  1101.5 4.5 copy-start.4
  1127.8 17.9 %copy-start.6 = (f32[100,256]{1,0:T(8,128)S(1)}, f32[100,256]{1,0:T(8,128)}, u32[]{:S(2)}) copy-start(f32[100,256]{1,0:T(8,128)} %copy-done.5) | copy-start | bytes 307204
  1127.8 17.9 %copy-start.9 = (f32[384]{0:T(512)S(1)}, f32[384]{0:T(512)}, u32[]{:S(2)}) copy-start(f32[384]{0:T(512)} %copy-done.8) | copy-start | bytes 4612
  1127.8 17.9 %copy-start.14 = (f32[1,1,256]{2,1,0:T(1,128)S(1)}, f32[1,1,256]{2,1,0:T(1,128)}, u32[]{:S(2)}) copy-start(f32[1,1,256]{2,1,0:T(1,128)} %param.16) | copy-start | bytes 3076
  1128.0 6.1 collective-permute-start.5
  1130.0 6.9 collective-permute-start.4
  1137.1 7.9 collective-permute-start.7
  1137.1 20.9 %copy-start.7 = (f32[100,256]{1,0:T(8,128)S(1)}, f32[100,256]{1,0:T(8,128)}, u32[]{:S(2)}) copy-start(f32[100,256]{1,0:T(8,128)} %get-tuple-element.76) | copy-start | bytes 307204
  1137.1 8.6 collective-permute-start.6
  1158.0 13.1 %copy-start.10 = (f32[1,1,256]{2,1,0:T(1,128)S(1)}, f32[1,1,256]{2,1,0:T(1,128)}, u32[]{:S(2)}) copy-start(f32[1,1,256]{2,1,0:T(1,128)} %param.15) | copy-start | bytes 3076
  1158.0 13.1 %copy-start.13 = (f32[52]{0:T(128)S(1)}, f32[52]{0:T(128)}, u32[]{:S(2)}) copy-start(f32[52]{0:T(128)} %copy-done.12) | copy-start | bytes 628
  1158.0 13.3 %copy-start.11 = (f32[1,1,256]{2,1,0:T(1,128)S(1)}, f32[1,1,256]{2,1,0:T(1,128)}, u32[]{:S(2)}) copy-start(f32[1,1,256]{2,1,0:T(1,128)} %param.17) | copy-start | bytes 3076
  (3 other events, 8.9 us)
